TPU v7x, 32 devices: a whole 2x2x4 slice. The times are simulated.
32 devices in a mesh: fsdp: 4 (over y, x), seq: 8 (over z, core).
Axes of the slice: x: 2, y: 2, z: 4, core: 2. Of those that a mesh axis runs over, the one named last changes fastest.
Arguments:
- image_input: bfloat16 [4, 1024, 1536], P('fsdp', 'seq'), may hold values from -6 to 6
- text_input: bfloat16 [4, 128, 1536], P('fsdp'), may hold values from -6 to 6
- w_qkv: bfloat16 [1536, 3, 2048], P('fsdp'), may hold values from -0.15625 to 0.15625
- query_gain: float32 [128], replicated, may hold values from 1.2 to 2.4
- key_gain: float32 [128], replicated, may hold values from 1.2 to 2.4
- image_cotangent: bfloat16 [4, 1024, 2048], P('fsdp', 'seq'), may hold values from -6 to 6
- text_cotangent: bfloat16 [4, 128, 2048], P('fsdp'), may hold values from -6 to 6
Outputs:
- image_grad: bfloat16 [4, 1024, 1536], P('fsdp', 'seq')
- text_grad: bfloat16 [4, 128, 1536], P('fsdp')
- weight_grad: float32 [1536, 3, 2048], P('fsdp', None, 'seq')
- gain_grad: float32 [2, 128], replicated
All inputs are finite; a program needn't handle non-finite values.
Results may differ from a plain program's by a relative error of at most 0.018.
The roundings to bfloat16 on the way count: a program that leaves them out, or rounds other values in their place, can miss the bound.
Values may be sent and summed in bfloat16 or wider, within the bound.
A program may use at most 192 MiB of HBM per device.

v0:
```python
import functools
import math

import jax
import jax.numpy as jnp
from jax import lax
from jax.experimental import pallas as pl
from jax.experimental.pallas import tpu as pltpu
from jax.sharding import PartitionSpec as P

EPSILON = 1e-06
MESH = pl.DeviceIdType.MESH
F32 = jnp.float32
BF16 = jnp.bfloat16
NT = (((1,), (1,)), ((), ()))


def kernel(
    nf, ns, image_ref, text_ref, weight_ref, up_ref, text_up_ref, qg_ref, kg_ref,
    image_out, text_out, weight_out, gain_out,
    tokens, weights, ups, triple, grads, qn_s, kn_s, knt_s, dq_s, dk_s, dv_s,
    sib_send, sib_recv, own_part, z_send, z_recv, w_send, w_recv, gain_all, gain_rows, text_half, tokens_t,
    x_send, x_recv, u_send, u_recv, wg_send, wg_recv, sb_send, sb_recv,
    zs_send, zs_recv, ws_send, ws_recv, g_send, g_recv, h_send, h_recv, t_send, t_recv, l_sem,
):
    f = lax.axis_index("fsdp")
    s = lax.axis_index("seq")
    nz = ns // 2
    z = lax.div(s, 2)
    core = lax.rem(s, 2)
    other = 1 - core
    sib = z * 2 + other
    rows = image_ref.shape[0]
    text_rows = text_ref.shape[0]
    parts, w_rows, all_width = weight_ref.shape
    own_width = all_width // ns
    head = qg_ref.shape[1]
    heads = own_width // head
    length = tokens.shape[0]
    piece = text_rows // ns

    def image_at(index, count=1):
        return pl.ds(pl.multiple_of(text_rows + index * rows, rows), count * rows)

    def remote(src, dst, send, recv, target):
        return pltpu.make_async_remote_copy(
            src_ref=src, dst_ref=dst, send_sem=send, recv_sem=recv,
            device_id=target, device_id_type=MESH,
        )

    barrier = pltpu.get_barrier_semaphore()
    for k in range(1, nf):
        pl.semaphore_signal(
            barrier, inc=1, device_id=(lax.rem(f + k, nf), s), device_id_type=MESH
        )
    for k in range(1, ns):
        pl.semaphore_signal(
            barrier, inc=1, device_id=(f, lax.rem(s + k, ns)), device_id_type=MESH
        )
    pl.semaphore_wait(barrier, nf + ns - 2)

    def x_copy(source, target_s, slot):
        return remote(
            image_ref if source is None else tokens.at[image_at(source)],
            tokens.at[image_at(s if source is None else source)],
            x_send.at[slot],
            x_recv.at[s if source is None else source],
            (f, target_s),
        )

    def w_at(index):
        return pl.ds(pl.multiple_of(index * w_rows, w_rows), w_rows)

    def u_at(index):
        return pl.ds(pl.multiple_of(index * own_width, own_width), own_width)

    own_rows = [
        pltpu.make_async_copy(
            weight_ref.at[c, :, u_at(s)],
            weights.at[w_at(f), pl.ds(c * own_width, own_width)],
            l_sem.at[4 + c],
        )
        for c in range(parts)
    ]
    for copy in own_rows:
        copy.start()
    sends = []
    for k in range(1, nz):
        sends.append(x_copy(None, lax.rem(z + k, nz) * 2 + core, k))
    sends.append(x_copy(None, sib, 0))
    for copy in sends:
        copy.start()
    for copy in own_rows:
        copy.wait()
    for k in range(1, nf):
        target = lax.rem(f + k, nf)
        sends.append(
            remote(
                weights.at[w_at(f)], weights.at[w_at(f)], wg_send.at[k], wg_recv.at[f],
                (target, s),
            )
        )
    for k in range(1, ns):
        target = lax.rem(s + k, ns)
        sends.append(
            remote(
                up_ref.at[:, u_at(target)], ups.at[image_at(s)], u_send.at[k], u_recv.at[s],
                (f, target),
            )
        )
    for copy in sends[nz:]:
        copy.start()
    locals_ = [
        pltpu.make_async_copy(image_ref, tokens.at[image_at(s)], l_sem.at[0]),
        pltpu.make_async_copy(text_ref, tokens.at[pl.ds(0, text_rows)], l_sem.at[1]),
        pltpu.make_async_copy(up_ref.at[:, u_at(s)], ups.at[image_at(s)], l_sem.at[2]),
        pltpu.make_async_copy(
            text_up_ref.at[:, u_at(s)], ups.at[pl.ds(0, text_rows)], l_sem.at[3]
        ),
    ]
    for copy in locals_:
        copy.start()
    for copy in locals_:
        copy.wait()
    for k in range(1, nf):
        source = lax.rem(f - k + nf, nf)
        remote(
            weights.at[w_at(f)], weights.at[w_at(source)], wg_send.at[k], wg_recv.at[source], (f, s)
        ).wait_recv()

    def project(at):
        tokens_t[:, at] = tokens[at, :].T
        triple[at, :] = jnp.dot(
            tokens[at, :], weights[...], preferred_element_type=F32
        ).astype(BF16)

    project(pl.ds(0, text_rows))
    forwards = []
    for k in range(nz):
        zt = lax.rem(z - k + nz, nz)
        if k:
            near = zt * 2 + core
            remote(
                image_ref, tokens.at[image_at(near)], x_send.at[k], x_recv.at[near], (f, s)
            ).wait_recv()
            forward = x_copy(near, sib, nz + k)
            forward.start()
            forwards.append(forward)
        far = zt * 2 + other
        remote(
            image_ref, tokens.at[image_at(far)], x_send.at[k], x_recv.at[far], (f, s)
        ).wait_recv()
        project(image_at(zt * 2, 2))
    for k in range(1, ns):
        source = lax.rem(s - k + ns, ns)
        remote(
            up_ref.at[:, u_at(s)], ups.at[image_at(source)], u_send.at[k], u_recv.at[source],
            (f, s),
        ).wait_recv()

    factor = 1.0 / math.sqrt(head)
    query_gain = qg_ref[...]
    key_gain = kg_ref[...]
    block = max(b for b in range(128, 385, 128) if length % b == 0)

    def columns(c, h):
        return pl.ds(c * own_width + h * head, head)

    def inverse_of(values):
        return lax.rsqrt(jnp.mean(values * values, axis=-1, keepdims=True) + EPSILON)

    def rms_backward(values, gain, incoming):
        inverse = inverse_of(values)
        weighted = incoming * gain
        inner = jnp.mean(weighted * values, axis=-1, keepdims=True)
        grad = inverse * weighted - values * (inverse * inverse * inverse * inner)
        return grad, jnp.sum(incoming * values * inverse, axis=0, keepdims=True)

    gain_q = jnp.zeros((1, head), F32)
    gain_k = jnp.zeros((1, head), F32)
    for h in range(heads):
        qf = triple[:, columns(0, h)].astype(F32)
        qn_s[...] = (qf * inverse_of(qf) * query_gain).astype(BF16)
        kf = triple[:, columns(1, h)].astype(F32)
        kn = (kf * inverse_of(kf) * key_gain).astype(BF16)
        kn_s[...] = kn
        knt_s[...] = kn.astype(F32).T.astype(BF16)
        dk_s[...] = jnp.zeros_like(dk_s)
        dv_s[...] = jnp.zeros_like(dv_s)

        def visit(i, carry, h=h):
            at = pl.ds(pl.multiple_of(i * block, block), block)
            queries = qn_s[at, :]
            upstream = ups[at, pl.ds(h * head, head)]
            scores = lax.dot_general(kn_s[...], queries, NT, preferred_element_type=F32)
            p = jnp.exp(scores * factor)
            p = p * (1.0 / jnp.sum(p, axis=0, keepdims=True))
            dp = lax.dot_general(
                triple[:, columns(2, h)], upstream, NT, preferred_element_type=F32
            )
            dot = jnp.sum(p * dp, axis=0, keepdims=True)
            ds = (p * (dp - dot)).astype(BF16)
            dv_s[...] += jnp.dot(p.astype(BF16), upstream, preferred_element_type=F32)
            dk_s[...] += jnp.dot(ds, queries, preferred_element_type=F32)
            dq_s[at, :] = jnp.dot(knt_s[...], ds, preferred_element_type=F32).T * factor
            return carry

        lax.fori_loop(0, length // block, visit, 0)
        dq, part = rms_backward(triple[:, columns(0, h)].astype(F32), query_gain, dq_s[...])
        gain_q += part
        grads[:, columns(0, h)] = dq.astype(BF16)
        dk, part = rms_backward(
            triple[:, columns(1, h)].astype(F32), key_gain, dk_s[...] * factor
        )
        gain_k += part
        grads[:, columns(1, h)] = dk.astype(BF16)
        grads[:, columns(2, h)] = dv_s[...].astype(BF16)

    gain_all[s, 0:1, :] = gain_q
    gain_all[s, 1:2, :] = gain_k
    for k in range(1, ns):
        copy = remote(
            gain_all.at[s], gain_all.at[s], g_send.at[k], g_recv.at[s], (f, lax.rem(s + k, ns))
        )
        copy.start()
        sends.append(copy)

    def text_at(index):
        return pl.ds(pl.multiple_of(index * piece, piece), piece)

    def share(at):
        return lax.dot_general(grads[at, :], weights[...], NT, preferred_element_type=F32)

    text_share = share(pl.ds(0, text_rows)).astype(BF16)
    text_half[...] = text_share
    siblings = []
    for k in range(nz):
        zt = lax.rem(z + k, nz)
        sib_send[k, pl.ds(0, rows), :] = share(image_at(zt * 2 + other)).astype(BF16)
        sib_send[k, pl.ds(rows, piece), :] = text_half[text_at(zt * 2 + other), :]
        copy = remote(
            sib_send.at[k], sib_recv.at[k], sb_send.at[k], sb_recv.at[k], (f, sib)
        )
        copy.start()
        siblings.append(copy)
    crossing = []
    for k in list(range(1, nz)) + [0]:
        zt = lax.rem(z + k, nz)
        mine = share(image_at(zt * 2 + core))
        siblings[k].wait_recv()
        total = mine + sib_recv[k, pl.ds(0, rows), :].astype(F32)
        text_total = text_half[text_at(zt * 2 + core), :].astype(F32) + sib_recv[
            k, pl.ds(rows, piece), :
        ].astype(F32)
        if k:
            z_send[k, pl.ds(0, rows), :] = total.astype(BF16)
            z_send[k, pl.ds(rows, piece), :] = text_total.astype(BF16)
            copy = remote(
                z_send.at[k], z_recv.at[k], zs_send.at[k], zs_recv.at[k], (f, zt * 2 + core)
            )
            copy.start()
            crossing.append(copy)
        else:
            own_part[pl.ds(0, rows), :] = total
            own_part[pl.ds(rows, piece), :] = text_total

    outgoing = []
    for k in list(range(1, nf)) + [0]:
        target = lax.rem(f + k, nf)
        at = pl.ds(pl.multiple_of(target * w_rows, w_rows), w_rows)
        term = jnp.dot(tokens_t[at, :], grads[...], preferred_element_type=F32)
        if k:
            w_send[k] = term.astype(BF16)
            copy = remote(
                w_send.at[k], w_recv.at[k], ws_send.at[k], ws_recv.at[k], (target, s)
            )
            copy.start()
            outgoing.append(copy)
        else:
            rounded = term.astype(BF16).astype(F32)
            for c in range(parts):
                weight_out[c] = rounded[:, c * own_width : (c + 1) * own_width]

    for k in range(1, ns):
        source = lax.rem(s - k + ns, ns)
        remote(
            gain_all.at[source], gain_all.at[source], g_send.at[k], g_recv.at[source], (f, s)
        ).wait_recv()
    gain = gain_all[0]
    for i in range(1, ns):
        gain += gain_all[i]
    gain_rows[f] = gain
    for k in range(1, nf):
        copy = remote(
            gain_rows.at[f], gain_rows.at[f], h_send.at[k], h_recv.at[f], (lax.rem(f + k, nf), s)
        )
        copy.start()
        sends.append(copy)
    for copy in crossing:
        copy.wait_recv()
    total = own_part[...]
    for k in range(1, nz):
        total += z_recv[k].astype(F32)
    image_out[...] = total[:rows].astype(BF16)
    text_out[text_at(s), :] = total[rows:].astype(BF16)
    texts = []
    for k in range(1, ns):
        target = lax.rem(s + k, ns)
        copy = remote(
            text_out.at[text_at(s)], text_out.at[text_at(s)], t_send.at[k], t_recv.at[s],
            (f, target),
        )
        copy.start()
        sends.append(copy)
    for copy in outgoing:
        copy.wait_recv()
    for k in range(1, nf):
        for c in range(parts):
            weight_out[c] += w_recv[k, :, c * own_width : (c + 1) * own_width].astype(F32)
    for k in range(1, nf):
        source = lax.rem(f - k + nf, nf)
        remote(
            gain_rows.at[source], gain_rows.at[source], h_send.at[k], h_recv.at[source], (f, s)
        ).wait_recv()
    gain = gain_rows[0]
    for i in range(1, nf):
        gain += gain_rows[i]
    gain_out[...] = gain
    for k in range(1, ns):
        source = lax.rem(s - k + ns, ns)
        remote(
            text_out.at[text_at(source)], text_out.at[text_at(source)], t_send.at[k],
            t_recv.at[source], (f, s),
        ).wait_recv()
    for copy in sends + forwards + siblings + crossing + outgoing:
        copy.wait_send()


def local(nf, ns, image_input, text_input, w_qkv, query_gain, key_gain, image_up, text_up):
    _, rows, depth = image_input.shape
    text_rows = text_input.shape[1]
    w_rows, three, all_width = w_qkv.shape
    own_width = all_width // ns
    head = query_gain.shape[0]
    length = text_rows + rows * ns
    nz = ns // 2
    width3 = three * own_width
    tall = rows + text_rows // ns
    vmem = pl.BlockSpec(memory_space=pltpu.VMEM)
    hbm = pl.BlockSpec(memory_space=pl.ANY)
    dma = pltpu.SemaphoreType.DMA
    image_grad, text_grad, weight_grad, gain = pl.pallas_call(
        functools.partial(kernel, nf, ns),
        out_shape=(
            jax.ShapeDtypeStruct((rows, depth), BF16),
            jax.ShapeDtypeStruct((text_rows, depth), BF16),
            jax.ShapeDtypeStruct((three, w_rows, own_width), F32),
            jax.ShapeDtypeStruct((8, head), F32),
        ),
        in_specs=[vmem, vmem, hbm, vmem, hbm, vmem, vmem],
        out_specs=(vmem,) * 4,
        scratch_shapes=[
            pltpu.VMEM((length, depth), BF16),
            pltpu.VMEM((depth, width3), BF16),
            pltpu.VMEM((length, own_width), BF16),
            pltpu.VMEM((length, width3), BF16),
            pltpu.VMEM((length, width3), BF16),
            pltpu.VMEM((length, head), BF16),
            pltpu.VMEM((length, head), BF16),
            pltpu.VMEM((head, length), BF16),
            pltpu.VMEM((length, head), F32),
            pltpu.VMEM((length, head), F32),
            pltpu.VMEM((length, head), F32),
            pltpu.VMEM((nz, tall, depth), BF16),
            pltpu.VMEM((nz, tall, depth), BF16),
            pltpu.VMEM((tall, depth), F32),
            pltpu.VMEM((nz, tall, depth), BF16),
            pltpu.VMEM((nz, tall, depth), BF16),
            pltpu.VMEM((nf, w_rows, width3), BF16),
            pltpu.VMEM((nf, w_rows, width3), BF16),
            pltpu.VMEM((ns, 8, head), F32),
            pltpu.VMEM((nf, 8, head), F32),
            pltpu.VMEM((text_rows, depth), BF16),
            pltpu.VMEM((depth, length), BF16),
            dma((2 * nz,)), dma((ns,)),
            dma((ns,)), dma((ns,)),
            dma((nf,)), dma((nf,)),
            dma((nz,)), dma((nz,)),
            dma((nz,)), dma((nz,)),
            dma((nf,)), dma((nf,)),
            dma((ns,)), dma((ns,)),
            dma((nf,)), dma((nf,)),
            dma((ns,)), dma((ns,)),
            dma((4 + three,)),
        ],
        compiler_params=pltpu.CompilerParams(
            collective_id=0, has_side_effects=True, vmem_limit_bytes=60 * 1024 * 1024
        ),
        name="joint_backward",
    )(
        image_input[0], text_input[0], w_qkv.transpose(1, 0, 2), image_up[0], text_up[0],
        query_gain.reshape(1, head), key_gain.reshape(1, head),
    )
    return (
        image_grad[None],
        text_grad[None],
        weight_grad.transpose(1, 0, 2),
        gain[:2],
    )


def solution(mesh):
    return jax.shard_map(
        functools.partial(local, mesh.shape["fsdp"], mesh.shape["seq"]),
        mesh=mesh,
        in_specs=(
            P("fsdp", "seq", None),
            P("fsdp", None, None),
            P("fsdp", None, None),
            P(),
            P(),
            P("fsdp", "seq", None),
            P("fsdp", None, None),
        ),
        out_specs=(P("fsdp", "seq", None), P("fsdp", None, None), P("fsdp", None, "seq"), P()),
        check_vma=False,
    )
```

profile of v0, /device:TPU:1, one launch (start us, length us, event | category | flops | bytes accessed | tf_op | source)
XLA Modules:
  0.0 129.7 jit_solution(10749864297162176938)
XLA Ops:
  0.6 123.1 %joint_backward.1 = (bf16[128,1536]{1,0:T(8,128)(2,1)}, bf16[128,1536]{1,0:T(8,128)(2,1)}, f32[3,384,256]{2,1,0:T(8,128)}, f32[8,128]{1,0:T(8,128)}) custom-call(bf16[128,1536]{1,0:T(8,128)(2,1)} %bitcast.16, bf16[128,1536]{1,0:T(8,128)(2,1)} %bitcast.17, bf16[3,384,2048]{2,1,0:T(8,128)(2,1)} %bitcast.10, bf16[128,2048]{1,0:T(8,128)(2,1)} %bitcast.12, ...), custom_call_target="tpu_custom_call" | custom-call | tf_op jit(solution)/shard_map/joint_backward/pallas_call | solution.py:352
  123.8 0.0 copy-start
  123.8 1.3 %slice.3 = f32[2,128]{1,0:T(2,128)} slice(f32[8,128]{1,0:T(8,128)} %get-tuple-element.11), slice={[0:2], [0:128]} | slice | bytes 2048 | tf_op jit(solution)/shard_map/slice | solution.py:408
  125.1 1.8 %copy.14 = bf16[1,128,1536]{2,1,0:T(8,128)(2,1)} copy(bf16[1,128,1536]{2,1,0:T(8,128)(2,1)} %bitcast.15) | data formatting | bytes 786432
  126.9 1.8 %copy.15 = bf16[1,128,1536]{2,1,0:T(8,128)(2,1)} copy(bf16[1,128,1536]{2,1,0:T(8,128)(2,1)} %bitcast.14) | data formatting | bytes 786432
  128.6 0.0 copy-done
  128.6 1.0 copy.16
Async XLA Ops:
  123.8 4.9 %copy-start = (f32[3,384,256]{2,1,0:T(8,128)S(1)}, f32[3,384,256]{2,1,0:T(8,128)}, u32[]{:S(2)}) copy-start(f32[3,384,256]{2,1,0:T(8,128)} %get-tuple-element.10) | copy-start | bytes 3538948
where the time goes:
time: 130 us
  Pallas kernels  123 us (95%)
  local copies, waits for them, and re-layouts  5.88 us (5%)
    pallas_call x1, Pallas kernels, local(): pl.pallas_call(functools.partial(kernel, nf, ns), out_shape=(jax.ShapeDty...  123 us
    unnamed x5, local copies, waits for them, and re-layouts  4.55 us

commit v1 on v0

v1 whole, which is shorter than its diff:
```python
import functools
import math

import jax
import jax.numpy as jnp
from jax import lax
from jax.experimental import pallas as pl
from jax.experimental.pallas import tpu as pltpu
from jax.sharding import PartitionSpec as P

EPSILON = 1e-06
MESH = pl.DeviceIdType.MESH
F32 = jnp.float32
BF16 = jnp.bfloat16
NT = (((1,), (1,)), ((), ()))
CHUNKS = 2


def kernel(
    nf, ns, image_ref, text_ref, weight_ref, up_ref, text_up_ref, qg_ref, kg_ref,
    image_out, text_out, weight_out, gain_out,
    tokens, weights, ups, triple, grads, qn_s, kn_s, knt_s, dq_s, dk_s, dv_s,
    sib_send, sib_recv, mine, line_send, line_recv, w_send, w_recv, gain_all, gain_rows,
    text_share, tokens_t,
    x_send, x_recv, u_send, u_recv, wg_send, wg_recv, sb_send, sb_recv,
    zs_send, zs_recv, ws_send, ws_recv, g_send, g_recv, h_send, h_recv, t_send, t_recv, l_sem,
):
    f = lax.axis_index("fsdp")
    s = lax.axis_index("seq")
    nz = ns // 2
    z = lax.div(s, 2)
    core = lax.rem(s, 2)
    other = 1 - core
    sib = z * 2 + other
    rows = image_ref.shape[0]
    text_rows = text_ref.shape[0]
    parts, w_rows, all_width = weight_ref.shape
    own_width = all_width // ns
    head = qg_ref.shape[1]
    heads = own_width // head
    length = tokens.shape[0]
    piece = text_rows // ns
    chunk = rows // CHUNKS
    half = w_rows // 2
    pending = []

    def remote(src, dst, send, recv, target):
        return pltpu.make_async_remote_copy(
            src_ref=src, dst_ref=dst, send_sem=send, recv_sem=recv,
            device_id=target, device_id_type=MESH,
        )

    def launch(copy, where=None):
        if where is None:
            copy.start()
        else:
            pl.when(where)(copy.start)
        pending.append((where, copy))

    def rank(at, who):
        away = jnp.abs(who - at)
        nearer = jnp.minimum(away - 1, at) + jnp.minimum(away - 1, nz - 1 - at)
        second = jnp.where((who > at) & (at >= away), 1, 0)
        return jnp.where(away == 0, 0, 1 + nearer + second)

    def place(at, who, which):
        return pl.multiple_of(text_rows + (rank(at, who) * 2 + which) * rows, rows)

    def w_at(index):
        return pl.ds(pl.multiple_of(index * w_rows, w_rows), w_rows)

    def u_at(index):
        return pl.ds(pl.multiple_of(index * own_width, own_width), own_width)

    own_at = pl.ds(place(z, z, core), rows)
    locals_ = [
        pltpu.make_async_copy(
            weight_ref.at[c, :, u_at(s)],
            weights.at[w_at(f), pl.ds(c * own_width, own_width)],
            l_sem.at[4 + c],
        )
        for c in range(parts)
    ] + [
        pltpu.make_async_copy(image_ref, tokens.at[own_at], l_sem.at[0]),
        pltpu.make_async_copy(text_ref, tokens.at[pl.ds(0, text_rows)], l_sem.at[1]),
        pltpu.make_async_copy(up_ref.at[:, u_at(s)], ups.at[own_at], l_sem.at[2]),
        pltpu.make_async_copy(
            text_up_ref.at[:, u_at(s)], ups.at[pl.ds(0, text_rows)], l_sem.at[3]
        ),
    ]
    for copy in locals_:
        copy.start()

    barrier = pltpu.get_barrier_semaphore()
    for k in range(1, nf):
        pl.semaphore_signal(
            barrier, inc=1, device_id=(lax.rem(f + k, nf), s), device_id_type=MESH
        )
    for k in range(1, ns):
        pl.semaphore_signal(
            barrier, inc=1, device_id=(f, lax.rem(s + k, ns)), device_id_type=MESH
        )
    pl.semaphore_wait(barrier, nf + ns - 2)

    up_ok = z < nz - 1
    down_ok = z > 0

    def x_copy(source, which, ch, to_z, to_core, own=False):
        src = (
            image_ref.at[pl.ds(ch * chunk, chunk)]
            if own
            else tokens.at[pl.ds(place(z, source, which) + ch * chunk, chunk)]
        )
        return remote(
            src,
            tokens.at[pl.ds(place(to_z, source, which) + ch * chunk, chunk)],
            x_send.at[len(x_count)],
            x_recv.at[rank(to_z, source) * 2 + which, ch],
            (f, to_z * 2 + to_core),
        )

    x_count = []

    def x_launch(*args, where=None, **kw):
        copy = x_copy(*args, **kw)
        x_count.append(0)
        launch(copy, where)

    def x_wait(source, which, ch):
        remote(
            image_ref.at[pl.ds(0, chunk)],
            tokens.at[pl.ds(place(z, source, which) + ch * chunk, chunk)],
            x_send.at[0], x_recv.at[rank(z, source) * 2 + which, ch], (f, s),
        ).wait_recv()

    for ch in range(CHUNKS):
        x_launch(z, core, ch, z + 1, core, own=True, where=up_ok)
        x_launch(z, core, ch, z - 1, core, own=True, where=down_ok)
        x_launch(z, core, ch, z, other, own=True)

    fast = lax.rem(f, 2)
    slow = lax.div(f, 2)
    na = nf // 2
    partner = slow * 2 + 1 - fast
    around = [lax.rem(slow + j, na) for j in range(1, na)]
    peers = [a * 2 + fast for a in around]
    corners = [a * 2 + 1 - fast for a in around]

    def w_half(source, hf):
        return weights.at[pl.ds(pl.multiple_of(source * w_rows + hf * half, half), half)]

    w_count = []

    def w_launch(source, hf, target):
        copy = remote(
            w_half(source, hf), w_half(source, hf), wg_send.at[len(w_count)],
            wg_recv.at[source, hf], (target, s),
        )
        w_count.append(0)
        launch(copy)

    def w_wait(source, hf):
        remote(
            w_half(f, hf), w_half(source, hf), wg_send.at[0], wg_recv.at[source, hf], (f, s)
        ).wait_recv()

    for copy in locals_[:parts]:
        copy.wait()
    w_launch(f, 0, partner)
    for q in peers:
        w_launch(f, 1, q)
    w_launch(f, 1, partner)
    for q in peers:
        w_launch(f, 0, q)
    for copy in locals_[parts:]:
        copy.wait()

    def relay_weights():
        w_wait(partner, 0)
        for q in peers:
            w_launch(partner, 0, q)
        for q in peers:
            w_wait(q, 1)
            w_launch(q, 1, partner)

    def finish_weights():
        w_wait(partner, 1)
        for q in peers:
            w_wait(q, 0)
        for q in corners:
            w_wait(q, 0)
            w_wait(q, 1)

    u_count = []

    def u_launch(to_z, to_core, h, where=None):
        column = (to_z * 2 + to_core) * own_width + h * head
        copy = remote(
            up_ref.at[:, pl.ds(pl.multiple_of(column, head), head)],
            ups.at[pl.ds(place(to_z, z, core), rows), pl.ds(h * head, head)],
            u_send.at[len(u_count)],
            u_recv.at[h, rank(to_z, z) * 2 + core],
            (f, to_z * 2 + to_core),
        )
        u_count.append(0)
        launch(copy, where)

    def send_upstream():
        for h in range(heads):
            u_launch(z, other, h)
            for d in range(1, nz):
                for which in (core, other):
                    u_launch(z + d, which, h, where=z + d < nz)
                    u_launch(z - d, which, h, where=z - d >= 0)

    def transpose(start, count):
        at = pl.ds(start, count)
        tokens_t[:, at] = tokens[at, :].T

    def project(start, count):
        at = pl.ds(start, count)
        triple[at, :] = jnp.dot(
            tokens[at, :], weights[...], preferred_element_type=F32
        ).astype(BF16)

    pair = 2 * rows
    first = text_rows + pair
    relayed = False
    for d in range(1, nz):
        sides = (
            (z - d, z - d >= 0, z + 1, up_ok),
            (z + d, z + d < nz, z - 1, down_ok),
        )
        if d == nz - 1:
            if not relayed:
                relay_weights()
                relayed = True
            for ch in range(CHUNKS):
                x_wait(z, other, ch)
            transpose(0, first)
            for k in range(1, nz - 1):
                transpose(first + (k - 1) * pair, pair)
            finish_weights()
            project(0, first)
            for k in range(1, nz - 1):
                project(first + (k - 1) * pair, pair)
        for ch in range(CHUNKS):
            for source, exists, onward, onward_ok in sides:
                pl.when(exists)(functools.partial(x_wait, source, core, ch))
                x_launch(source, core, ch, onward, core, where=exists & onward_ok)
                x_launch(source, core, ch, z, other, where=exists)
            if not relayed:
                relay_weights()
                relayed = True
        for ch in range(CHUNKS):
            for source, exists, onward, onward_ok in sides:
                pl.when(exists)(functools.partial(x_wait, source, other, ch))
        if d == max(1, nz - 2):
            send_upstream()
    last = first + (nz - 2) * pair
    transpose(last, pair)
    project(last, pair)

    factor = 1.0 / math.sqrt(head)
    query_gain = qg_ref[...]
    key_gain = kg_ref[...]
    block = max(b for b in range(128, 385, 128) if length % b == 0)
    per_block = block // rows
    text_pieces = text_rows // rows

    def columns(c, h):
        return pl.ds(c * own_width + h * head, head)

    def inverse_of(values):
        return lax.rsqrt(jnp.mean(values * values, axis=-1, keepdims=True) + EPSILON)

    def rms_backward(values, gain, incoming):
        inverse = inverse_of(values)
        weighted = incoming * gain
        inner = jnp.mean(weighted * values, axis=-1, keepdims=True)
        grad = inverse * weighted - values * (inverse * inverse * inverse * inner)
        return grad, jnp.sum(incoming * values * inverse, axis=0, keepdims=True)

    def u_wait(h, j):
        at = pl.ds(pl.multiple_of(text_rows + j * rows, rows), rows)
        remote(
            up_ref.at[:, pl.ds(0, head)],
            ups.at[at, pl.ds(h * head, head)],
            u_send.at[0], u_recv.at[h, j], (f, s),
        ).wait_recv()

    gain_q = jnp.zeros((1, head), F32)
    gain_k = jnp.zeros((1, head), F32)
    for h in range(heads):
        qf = triple[:, columns(0, h)].astype(F32)
        qn_s[...] = (qf * inverse_of(qf) * query_gain).astype(BF16)
        kf = triple[:, columns(1, h)].astype(F32)
        kn = (kf * inverse_of(kf) * key_gain).astype(BF16)
        kn_s[...] = kn
        knt_s[...] = kn.astype(F32).T.astype(BF16)
        dk_s[...] = jnp.zeros_like(dk_s)
        dv_s[...] = jnp.zeros_like(dv_s)

        def visit(i, carry, h=h):
            for jj in range(per_block):
                j = i * per_block + jj - text_pieces
                pl.when((j >= 0) & (j != core))(functools.partial(u_wait, h, j))
            at = pl.ds(pl.multiple_of(i * block, block), block)
            queries = qn_s[at, :]
            upstream = ups[at, pl.ds(h * head, head)]
            scores = lax.dot_general(kn_s[...], queries, NT, preferred_element_type=F32)
            p = jnp.exp(scores * factor)
            p = p * (1.0 / jnp.sum(p, axis=0, keepdims=True))
            dp = lax.dot_general(
                triple[:, columns(2, h)], upstream, NT, preferred_element_type=F32
            )
            dot = jnp.sum(p * dp, axis=0, keepdims=True)
            ds = (p * (dp - dot)).astype(BF16)
            dv_s[...] += jnp.dot(p.astype(BF16), upstream, preferred_element_type=F32)
            dk_s[...] += jnp.dot(ds, queries, preferred_element_type=F32)
            dq_s[at, :] = jnp.dot(knt_s[...], ds, preferred_element_type=F32).T * factor
            return carry

        lax.fori_loop(0, length // block, visit, 0)
        dq, part = rms_backward(triple[:, columns(0, h)].astype(F32), query_gain, dq_s[...])
        gain_q += part
        grads[:, columns(0, h)] = dq.astype(BF16)
        dk, part = rms_backward(
            triple[:, columns(1, h)].astype(F32), key_gain, dk_s[...] * factor
        )
        gain_k += part
        grads[:, columns(1, h)] = dk.astype(BF16)
        grads[:, columns(2, h)] = dv_s[...].astype(BF16)

    gain_all[s, 0:1, :] = gain_q
    gain_all[s, 1:2, :] = gain_k
    for k in range(1, ns):
        launch(
            remote(
                gain_all.at[s], gain_all.at[s], g_send.at[k], g_recv.at[s],
                (f, lax.rem(s + k, ns)),
            )
        )

    def text_at(index):
        return pl.ds(pl.multiple_of(index * piece, piece), piece)

    def share(at):
        return lax.dot_general(grads[at, :], weights[...], NT, preferred_element_type=F32)

    text_share[...] = share(pl.ds(0, text_rows))
    cuts = ((0, piece + chunk), (piece + chunk, rows - chunk))
    ends = (z == 0) | (z == nz - 1)
    middle = (z > 0) & (z < nz - 1)

    def ordered(k):
        return jnp.where(2 * z < nz, nz - 1 - k, k)

    def fill(k):
        zt = ordered(k)
        value = share(pl.ds(place(z, zt, 0), pair))
        low, high = value[:rows], value[rows:]
        here = core == 0
        mine[zt, pl.ds(piece, rows), :] = jnp.where(here, low, high)
        mine[zt, pl.ds(0, piece), :] = text_share[text_at(zt * 2 + core), :]
        sib_send[zt, pl.ds(piece, rows), :] = jnp.where(here, high, low).astype(BF16)
        sib_send[zt, pl.ds(0, piece), :] = text_share[text_at(zt * 2 + other), :].astype(BF16)
        launch(
            remote(sib_send.at[zt], sib_recv.at[zt], sb_send.at[zt], sb_recv.at[zt], (f, sib))
        )

    def sib_wait(zt):
        remote(
            sib_send.at[zt], sib_recv.at[zt], sb_send.at[zt], sb_recv.at[zt], (f, s)
        ).wait_recv()

    def combined(zt, cut):
        at = pl.ds(*cut)
        return mine[zt, at, :] + sib_recv[zt, at, :].astype(F32)

    def line_copy(zt, ch, to_z):
        slot = jnp.where((to_z < z) & (zt == to_z), nz, zt)
        at = pl.ds(*cuts[ch])
        return remote(
            line_send.at[zt, at], line_recv.at[slot, at], zs_send.at[zt, ch],
            zs_recv.at[slot, ch], (f, to_z * 2 + core),
        )

    def line_wait(slot, ch):
        at = pl.ds(*cuts[ch])
        remote(
            line_send.at[0, at], line_recv.at[slot, at], zs_send.at[0, ch],
            zs_recv.at[slot, ch], (f, s),
        ).wait_recv()

    def originate(k):
        zt = ordered(k)
        sib_wait(zt)
        for ch in range(CHUNKS):
            line_send[zt, pl.ds(*cuts[ch]), :] = combined(zt, cuts[ch]).astype(BF16)
            line_copy(zt, ch, jnp.where(z == 0, 1, nz - 2)).start()

    def pass_on(zt, ch, to_z):
        at = pl.ds(*cuts[ch])
        line_wait(zt, ch)
        total = combined(zt, cuts[ch]) + line_recv[zt, at, :].astype(F32)
        line_send[zt, at, :] = total.astype(BF16)
        line_copy(zt, ch, to_z).start()

    targets = [partner] + peers + corners

    def term(k):
        target = f if k == nf - 1 else targets[k]
        value = jnp.dot(tokens_t[w_at(target), :], grads[...], preferred_element_type=F32)
        if k < nf - 1:
            w_send[k] = value.astype(BF16)
            launch(
                remote(w_send.at[k], w_recv.at[f], ws_send.at[k], ws_recv.at[f], (target, s))
            )
        else:
            rounded = value.astype(BF16).astype(F32)
            for c in range(parts):
                weight_out[c] = rounded[:, c * own_width : (c + 1) * own_width]

    fill(0)
    for k in range(1, nz):
        fill(k)
        pl.when(ends)(functools.partial(originate, k - 1))
        if k <= nf:
            term(k - 1)
    for k in range(nz - 1, nf):
        term(k)

    for k in range(1, ns):
        source = lax.rem(s - k + ns, ns)
        remote(
            gain_all.at[source], gain_all.at[source], g_send.at[k], g_recv.at[source], (f, s)
        ).wait_recv()
    gain = gain_all[0]
    for i in range(1, ns):
        gain += gain_all[i]
    gain_rows[f] = gain
    for k in range(1, nf):
        launch(
            remote(
                gain_rows.at[f], gain_rows.at[f], h_send.at[k], h_recv.at[f],
                (lax.rem(f + k, nf), s),
            )
        )

    @pl.when(middle)
    def _():
        for k in range(nz):
            sib_wait(ordered(k))
        for t in range(nz - 1):
            for ch in range(CHUNKS):
                down = t - (nz - 1) + z
                pl.when(down >= 0)(functools.partial(pass_on, down, ch, z - 1))
                pl.when(t >= z)(functools.partial(pass_on, nz - 1 + z - t, ch, z + 1))

    pl.when(ends)(functools.partial(sib_wait, z))

    def finish(ch):
        at = pl.ds(*cuts[ch])

        def arrived(slot):
            line_wait(slot, ch)
            mine[z, at, :] += line_recv[slot, at, :].astype(F32)

        pl.when(down_ok)(functools.partial(arrived, z))
        pl.when(up_ok)(functools.partial(arrived, nz))
        total = combined(z, cuts[ch]).astype(BF16)
        if ch == 0:
            text_out[text_at(s), :] = total[:piece]
            image_out[pl.ds(0, chunk), :] = total[piece:]
        else:
            image_out[pl.ds(chunk, rows - chunk), :] = total

    t_count = []

    def t_launch(index, to_z, to_core):
        at = text_at(index)
        copy = remote(
            text_out.at[at], text_out.at[at], t_send.at[len(t_count)], t_recv.at[index],
            (f, to_z * 2 + to_core),
        )
        t_count.append(0)
        launch(copy)

    def t_wait(index):
        at = text_at(index)
        remote(
            text_out.at[at], text_out.at[at], t_send.at[0], t_recv.at[index], (f, s)
        ).wait_recv()

    finish(0)
    for k in range(1, nz):
        t_launch(s, lax.rem(z + k, nz), core)
    t_launch(s, z, other)

    for q in targets:
        remote(
            w_send.at[0], w_recv.at[q], ws_send.at[0], ws_recv.at[q], (f, s)
        ).wait_recv()
        for c in range(parts):
            weight_out[c] += w_recv[q, :, c * own_width : (c + 1) * own_width].astype(F32)
    for k in range(1, nf):
        source = lax.rem(f - k + nf, nf)
        remote(
            gain_rows.at[source], gain_rows.at[source], h_send.at[k], h_recv.at[source], (f, s)
        ).wait_recv()
    gain = gain_rows[0]
    for i in range(1, nf):
        gain += gain_rows[i]
    gain_out[...] = gain[:2]

    for k in range(1, nz):
        near = lax.rem(z - k + nz, nz) * 2 + core
        t_wait(near)
        t_launch(near, z, other)
    finish(1)
    for k in range(nz):
        t_wait(lax.rem(z + k, nz) * 2 + other)

    for where, copy in pending:
        if where is None:
            copy.wait_send()
        else:
            pl.when(where)(copy.wait_send)
    for ch in range(CHUNKS):
        for k in range(nz - 1):
            pl.when(ends)(line_copy(ordered(k), ch, jnp.where(z == 0, 1, nz - 2)).wait_send)

            def sent(zt, ch=ch):
                pl.when(zt != z)(line_copy(zt, ch, z).wait_send)

        for k in range(nz):
            pl.when(middle)(functools.partial(sent, k))


def emit(*refs):
    sems = refs[-1]
    count = len(refs) // 2
    copies = [
        pltpu.make_async_copy(refs[i], refs[count + i], sems.at[i]) for i in range(count)
    ]
    for copy in copies:
        copy.start()
    for copy in copies:
        copy.wait()


def local(nf, ns, image_input, text_input, w_qkv, query_gain, key_gain, image_up, text_up):
    _, rows, depth = image_input.shape
    text_rows = text_input.shape[1]
    w_rows, three, all_width = w_qkv.shape
    own_width = all_width // ns
    head = query_gain.shape[0]
    heads = own_width // head
    length = text_rows + rows * ns
    nz = ns // 2
    width3 = three * own_width
    tall = rows + text_rows // ns
    vmem = pl.BlockSpec(memory_space=pltpu.VMEM)
    hbm = pl.BlockSpec(memory_space=pl.ANY)
    dma = pltpu.SemaphoreType.DMA
    results = pl.pallas_call(
        functools.partial(kernel, nf, ns),
        out_shape=(
            pltpu.VMEM((rows, depth), BF16),
            pltpu.VMEM((text_rows, depth), BF16),
            pltpu.VMEM((three, w_rows, own_width), F32),
            pltpu.VMEM((2, head), F32),
        ),
        in_specs=[hbm, hbm, hbm, hbm, hbm, vmem, vmem],
        out_specs=(vmem,) * 4,
        scratch_shapes=[
            pltpu.VMEM((length, depth), BF16),
            pltpu.VMEM((depth, width3), BF16),
            pltpu.VMEM((length, own_width), BF16),
            pltpu.VMEM((length, width3), BF16),
            pltpu.VMEM((length, width3), BF16),
            pltpu.VMEM((length, head), BF16),
            pltpu.VMEM((length, head), BF16),
            pltpu.VMEM((head, length), BF16),
            pltpu.VMEM((length, head), F32),
            pltpu.VMEM((length, head), F32),
            pltpu.VMEM((length, head), F32),
            pltpu.VMEM((nz, tall, depth), BF16),
            pltpu.VMEM((nz, tall, depth), BF16),
            pltpu.VMEM((nz, tall, depth), F32),
            pltpu.VMEM((nz, tall, depth), BF16),
            pltpu.VMEM((nz + 1, tall, depth), BF16),
            pltpu.VMEM((nf - 1, w_rows, width3), BF16),
            pltpu.VMEM((nf, w_rows, width3), BF16),
            pltpu.VMEM((ns, 8, head), F32),
            pltpu.VMEM((nf, 8, head), F32),
            pltpu.VMEM((text_rows, depth), F32),
            pltpu.VMEM((depth, length), BF16),
            dma((3 * CHUNKS + 4 * (nz - 1) * CHUNKS,)), dma((ns, CHUNKS)),
            dma((heads * (1 + 4 * (nz - 1)),)), dma((heads, ns)),
            dma((2 + 4 * (nf // 2 - 1),)), dma((nf, 2)),
            dma((nz,)), dma((nz,)),
            dma((nz, CHUNKS)), dma((nz + 1, CHUNKS)),
            dma((nf,)), dma((nf,)),
            dma((ns,)), dma((ns,)),
            dma((nf,)), dma((nf,)),
            dma((2 * nz,)), dma((ns,)),
            dma((4 + three,)),
        ],
        compiler_params=pltpu.CompilerParams(
            collective_id=0, has_side_effects=True, vmem_limit_bytes=56 * 1024 * 1024
        ),
        name="joint_backward",
    )(
        image_input[0], text_input[0], w_qkv.transpose(1, 0, 2), image_up[0], text_up[0],
        query_gain.reshape(1, head), key_gain.reshape(1, head),
    )
    image_grad, text_grad, weight_grad, gain = pl.pallas_call(
        emit,
        out_shape=tuple(jax.ShapeDtypeStruct(r.shape, r.dtype) for r in results),
        in_specs=[hbm] * 4,
        out_specs=(hbm,) * 4,
        scratch_shapes=[dma((4,))],
        compiler_params=pltpu.CompilerParams(vmem_limit_bytes=1024 * 1024),
        name="emit",
    )(*results)
    return (
        image_grad[None],
        text_grad[None],
        weight_grad.transpose(1, 0, 2),
        gain,
    )


def solution(mesh):
    return jax.shard_map(
        functools.partial(local, mesh.shape["fsdp"], mesh.shape["seq"]),
        mesh=mesh,
        in_specs=(
            P("fsdp", "seq", None),
            P("fsdp", None, None),
            P("fsdp", None, None),
            P(),
            P(),
            P("fsdp", "seq", None),
            P("fsdp", None, None),
        ),
        out_specs=(P("fsdp", "seq", None), P("fsdp", None, None), P("fsdp", None, "seq"), P()),
        check_vma=False,
    )
```

time: 130 us -> 94.9 us (0.73)
  Pallas kernels: 123 us -> 93.9 us
  local copies, waits for them, and re-layouts: 5.88 us -> 0 us
    pallas_call x1 -> x2, Pallas kernels: 123 us -> 93.9 us  [the longest x1 92.6 us: local(): pl.pallas_call(functools.partial(kernel, nf, ns), out_shape=(pltpu.VMEM((...]
    unnamed x5 -> x0, local copies, waits for them, and re-layouts: 4.55 us -> none
    slice x1 -> x0, local copies, waits for them, and re-layouts: 1.33 us -> none  [local(): gain[:2]]
where the time goes in v1:
time: 94.9 us; the launch traced here: 94.7 us
  Pallas kernels  93.9 us (99%)
    pallas_call x1, Pallas kernels, local(): pl.pallas_call(functools.partial(kernel, nf, ns), out_shape=(pltpu.VMEM((...  92.6 us

profile of v1, /device:TPU:1, one launch (start us, length us, event | category | flops | bytes accessed | tf_op | source)
XLA Modules:
  0.0 94.7 jit_solution(14538611914270284774)
XLA Ops:
  0.6 92.6 %joint_backward.1 = (bf16[128,1536]{1,0:T(8,128)(2,1)S(1)}, bf16[128,1536]{1,0:T(8,128)(2,1)S(1)}, f32[3,384,256]{2,1,0:T(8,128)S(1)}, f32[2,128]{1,0:T(2,128)S(1)}) custom-call(bf16[128,1536]{1,0:T(8,128)(2,1)} %bitcast.13, bf16[128,1536]{1,0:T(8,128)(2,1)} %bitcast.14, bf16[3,384,2048]{2,1,0:T(8,128)(2,1)} %bitcast.10, bf16[128,2048]{1,0:T(8,128)(2,1)} %bitcast.11, ...), custom_call_target="tpu_custom_call" | custom-call | tf_op jit(solution)/shard_map/joint_backward/pallas_call | solution.py:567
  93.2 1.3 %emit.1 = (bf16[128,1536]{1,0:T(8,128)(2,1)}, bf16[128,1536]{1,0:T(8,128)(2,1)}, f32[3,384,256]{2,1,0:T(8,128)}, f32[2,128]{1,0:T(2,128)}) custom-call(bf16[128,1536]{1,0:T(8,128)(2,1)S(1)} %get-tuple-element.12.refs_0_, bf16[128,1536]{1,0:T(8,128)(2,1)S(1)} %get-tuple-element.13.refs_1_, f32[3,384,256]{2,1,0:T(8,128)S(1)} %get-tuple-element.14.refs_2_, ...), custom_call_target="tpu_custom_call" | custom-call | tf_op jit(solution)/shard_map/emit/pallas_call | solution.py:619

commit v2 on v1

--- a/solution.py
+++ b/solution.py
@@ -21,9 +21,10 @@
     image_out, text_out, weight_out, gain_out,
     tokens, weights, ups, triple, grads, qn_s, kn_s, knt_s, dq_s, dk_s, dv_s,
     sib_send, sib_recv, mine, line_send, line_recv, w_send, w_recv, gain_all, gain_rows,
-    text_share, tokens_t,
+    text_share, text_sib_send, text_sib_recv, text_send, text_recv, tokens_t,
     x_send, x_recv, u_send, u_recv, wg_send, wg_recv, sb_send, sb_recv,
-    zs_send, zs_recv, ws_send, ws_recv, g_send, g_recv, h_send, h_recv, t_send, t_recv, l_sem,
+    zs_send, zs_recv, ws_send, ws_recv, g_send, g_recv, h_send, h_recv, t_send, t_recv,
+    ts_send, ts_recv, tz_send, tz_recv, l_sem,
 ):
     f = lax.axis_index("fsdp")
     s = lax.axis_index("seq")
@@ -39,7 +40,7 @@
     head = qg_ref.shape[1]
     heads = own_width // head
     length = tokens.shape[0]
-    piece = text_rows // ns
+    piece = text_rows // 4
     chunk = rows // CHUNKS
     half = w_rows // 2
     pending = []
@@ -349,22 +350,81 @@
         return lax.dot_general(grads[at, :], weights[...], NT, preferred_element_type=F32)
 
     text_share[...] = share(pl.ds(0, text_rows))
-    cuts = ((0, piece + chunk), (piece + chunk, rows - chunk))
+    cuts = [(ch * chunk, chunk) for ch in range(CHUNKS)]
     ends = (z == 0) | (z == nz - 1)
     middle = (z > 0) & (z < nz - 1)
 
     def ordered(k):
         return jnp.where(2 * z < nz, nz - 1 - k, k)
+
+    def text_swap():
+        for o in range(2):
+            text_sib_send[o] = text_share[text_at(o * 2 + other), :].astype(BF16)
+        return remote(
+            text_sib_send, text_sib_recv, ts_send.at[0], ts_recv.at[0], (f, sib)
+        )
+
+    swap = text_swap()
+    launch(swap)
+
+    def text_line(o, direction):
+        return remote(
+            text_send.at[o], text_recv.at[1 - direction, o], tz_send.at[o],
+            tz_recv.at[1 - direction, o], (f, (z - 1 + 2 * direction) * 2 + core),
+        )
+
+    def t_copy(index, to_z, to_core, slot):
+        at = text_at(index)
+        return remote(
+            text_out.at[at], text_out.at[at], t_send.at[slot], t_recv.at[index],
+            (f, to_z * 2 + to_core),
+        )
+
+    def own_text():
+        index = (z - (nz // 2 - 1)) * 2 + core
+        copies = [t_copy(index, lax.rem(z + k, nz), core, k) for k in range(1, nz)]
+        return copies + [t_copy(index, z, other, 0)]
+
+    def text_step(k):
+        o = jnp.where(2 * z < nz, 1 - k, k)
+        owner = nz // 2 - 1 + o
+        at = text_at(o * 2 + core)
+        text_share[at, :] += text_sib_recv[o].astype(F32)
+
+        def arrived(side):
+            remote(
+                text_send.at[0], text_recv.at[side, o], tz_send.at[0], tz_recv.at[side, o],
+                (f, s),
+            ).wait_recv()
+            text_share[at, :] += text_recv[side, o].astype(F32)
+
+        pl.when((z > 0) & (z <= owner))(functools.partial(arrived, 0))
+        pl.when((z < nz - 1) & (z >= owner))(functools.partial(arrived, 1))
+        total = text_share[at, :].astype(BF16)
+
+        @pl.when(z != owner)
+        def _():
+            text_send[o] = total
+            text_line(o, jnp.where(z < owner, 1, 0)).start()
+
+        @pl.when(z == owner)
+        def _():
+            text_out[at, :] = total
+            for copy in own_text():
+                copy.start()
+
+    def text_steps():
+        swap.wait_recv()
+        for k in range(2):
+            text_step(k)
 
     def fill(k):
         zt = ordered(k)
         value = share(pl.ds(place(z, zt, 0), pair))
         low, high = value[:rows], value[rows:]
         here = core == 0
-        mine[zt, pl.ds(piece, rows), :] = jnp.where(here, low, high)
-        mine[zt, pl.ds(0, piece), :] = text_share[text_at(zt * 2 + core), :]
-        sib_send[zt, pl.ds(piece, rows), :] = jnp.where(here, high, low).astype(BF16)
-        sib_send[zt, pl.ds(0, piece), :] = text_share[text_at(zt * 2 + other), :].astype(BF16)
+        mine[zt] = jnp.where(here, low, high)
+        sib_send[zt] = jnp.where(here, high, low).astype(BF16)
         launch(
             remote(sib_send.at[zt], sib_recv.at[zt], sb_send.at[zt], sb_recv.at[zt], (f, sib))
         )
@@ -423,6 +483,7 @@
                 weight_out[c] = rounded[:, c * own_width : (c + 1) * own_width]
 
     fill(0)
+    pl.when(ends)(text_steps)
     for k in range(1, nz):
         fill(k)
         pl.when(ends)(functools.partial(originate, k - 1))
@@ -450,6 +511,7 @@
 
     @pl.when(middle)
     def _():
+        text_steps()
         for k in range(nz):
             sib_wait(ordered(k))
         for t in range(nz - 1):
@@ -469,35 +531,21 @@
 
         pl.when(down_ok)(functools.partial(arrived, z))
         pl.when(up_ok)(functools.partial(arrived, nz))
-        total = combined(z, cuts[ch]).astype(BF16)
-        if ch == 0:
-            text_out[text_at(s), :] = total[:piece]
-            image_out[pl.ds(0, chunk), :] = total[piece:]
-        else:
-            image_out[pl.ds(chunk, rows - chunk), :] = total
-
-    t_count = []
-
-    def t_launch(index, to_z, to_core):
-        at = text_at(index)
-        copy = remote(
-            text_out.at[at], text_out.at[at], t_send.at[len(t_count)], t_recv.at[index],
-            (f, to_z * 2 + to_core),
-        )
-        t_count.append(0)
-        launch(copy)
+        image_out[at, :] = combined(z, cuts[ch]).astype(BF16)
 
     def t_wait(index):
-        at = text_at(index)
-        remote(
-            text_out.at[at], text_out.at[at], t_send.at[0], t_recv.at[index], (f, s)
-        ).wait_recv()
+        t_copy(index, z, core, 0).wait_recv()
+
+    center = nz // 2 - 1
+    for o in range(2):
+        index = o * 2 + core
+
+        @pl.when(z != center + o)
+        def _(index=index, o=o):
+            t_wait(index)
+            t_copy(index, z, other, nz + o).start()
 
     finish(0)
-    for k in range(1, nz):
-        t_launch(s, lax.rem(z + k, nz), core)
-    t_launch(s, z, other)
-
     for q in targets:
         remote(
             w_send.at[0], w_recv.at[q], ws_send.at[0], ws_recv.at[q], (f, s)
@@ -514,13 +562,10 @@
         gain += gain_rows[i]
     gain_out[...] = gain[:2]
 
-    for k in range(1, nz):
-        near = lax.rem(z - k + nz, nz) * 2 + core
-        t_wait(near)
-        t_launch(near, z, other)
-    finish(1)
-    for k in range(nz):
-        t_wait(lax.rem(z + k, nz) * 2 + other)
+    for ch in range(1, CHUNKS):
+        finish(ch)
+    for o in range(2):
+        t_wait(o * 2 + other)
 
     for where, copy in pending:
         if where is None:
@@ -536,6 +581,15 @@
 
         for k in range(nz):
             pl.when(middle)(functools.partial(sent, k))
+    for o in range(2):
+        owner = center + o
+        pl.when(z != owner)(text_line(o, jnp.where(z < owner, 1, 0)).wait_send)
+        pl.when(z != owner)(t_copy(o * 2 + core, z, other, nz + o).wait_send)
+
+    @pl.when((z == center) | (z == center + 1))
+    def _():
+        for copy in own_text():
+            copy.wait_send()
 
 
 def emit(*refs):
@@ -560,7 +614,7 @@
     length = text_rows + rows * ns
     nz = ns // 2
     width3 = three * own_width
-    tall = rows + text_rows // ns
+    piece = text_rows // 4
     vmem = pl.BlockSpec(memory_space=pltpu.VMEM)
     hbm = pl.BlockSpec(memory_space=pl.ANY)
     dma = pltpu.SemaphoreType.DMA
@@ -586,16 +640,20 @@
             pltpu.VMEM((length, head), F32),
             pltpu.VMEM((length, head), F32),
             pltpu.VMEM((length, head), F32),
-            pltpu.VMEM((nz, tall, depth), BF16),
-            pltpu.VMEM((nz, tall, depth), BF16),
-            pltpu.VMEM((nz, tall, depth), F32),
-            pltpu.VMEM((nz, tall, depth), BF16),
-            pltpu.VMEM((nz + 1, tall, depth), BF16),
+            pltpu.VMEM((nz, rows, depth), BF16),
+            pltpu.VMEM((nz, rows, depth), BF16),
+            pltpu.VMEM((nz, rows, depth), F32),
+            pltpu.VMEM((nz, rows, depth), BF16),
+            pltpu.VMEM((nz + 1, rows, depth), BF16),
             pltpu.VMEM((nf - 1, w_rows, width3), BF16),
             pltpu.VMEM((nf, w_rows, width3), BF16),
             pltpu.VMEM((ns, 8, head), F32),
             pltpu.VMEM((nf, 8, head), F32),
             pltpu.VMEM((text_rows, depth), F32),
+            pltpu.VMEM((2, piece, depth), BF16),
+            pltpu.VMEM((2, piece, depth), BF16),
+            pltpu.VMEM((2, piece, depth), BF16),
+            pltpu.VMEM((2, 2, piece, depth), BF16),
             pltpu.VMEM((depth, length), BF16),
             dma((3 * CHUNKS + 4 * (nz - 1) * CHUNKS,)), dma((ns, CHUNKS)),
             dma((heads * (1 + 4 * (nz - 1)),)), dma((heads, ns)),
@@ -605,7 +663,8 @@
             dma((nf,)), dma((nf,)),
             dma((ns,)), dma((ns,)),
             dma((nf,)), dma((nf,)),
-            dma((2 * nz,)), dma((ns,)),
+            dma((nz + 2,)), dma((4,)),
+            dma((1,)), dma((1,)), dma((2,)), dma((2, 2)),
             dma((4 + three,)),
         ],
         compiler_params=pltpu.CompilerParams(

time: 94.9 us -> 90.9 us (0.958); the launches traced: 94.7 us -> 89.4 us
  Pallas kernels: 93.9 us -> 88.6 us
    pallas_call x1, Pallas kernels: 92.6 us -> 87.3 us  [local(): pl.pallas_call(functools.partial(kernel, nf, ns), out_shape=(pltpu.VMEM((...]
where the time goes in v2:
time: 90.9 us; the launch traced here: 89.4 us
  Pallas kernels  88.6 us (97%)
    pallas_call x1, Pallas kernels, local(): pl.pallas_call(functools.partial(kernel, nf, ns), out_shape=(pltpu.VMEM((...  87.3 us

profile of v2, /device:TPU:1, one launch (start us, length us, event | category | flops | bytes accessed | tf_op | source)
XLA Modules:
  0.0 89.4 jit_solution(2494430715431128153)
XLA Ops:
  0.6 87.3 %joint_backward.1 = (bf16[128,1536]{1,0:T(8,128)(2,1)S(1)}, bf16[128,1536]{1,0:T(8,128)(2,1)S(1)}, f32[3,384,256]{2,1,0:T(8,128)S(1)}, f32[2,128]{1,0:T(2,128)S(1)}) custom-call(bf16[128,1536]{1,0:T(8,128)(2,1)} %bitcast.13, bf16[128,1536]{1,0:T(8,128)(2,1)} %bitcast.14, bf16[3,384,2048]{2,1,0:T(8,128)(2,1)} %bitcast.10, bf16[128,2048]{1,0:T(8,128)(2,1)} %bitcast.11, ...), custom_call_target="tpu_custom_call" | custom-call | tf_op jit(solution)/shard_map/joint_backward/pallas_call | solution.py:621
  87.9 1.3 %emit.1 = (bf16[128,1536]{1,0:T(8,128)(2,1)}, bf16[128,1536]{1,0:T(8,128)(2,1)}, f32[3,384,256]{2,1,0:T(8,128)}, f32[2,128]{1,0:T(2,128)}) custom-call(bf16[128,1536]{1,0:T(8,128)(2,1)S(1)} %get-tuple-element.12.refs_0_, bf16[128,1536]{1,0:T(8,128)(2,1)S(1)} %get-tuple-element.13.refs_1_, f32[3,384,256]{2,1,0:T(8,128)S(1)} %get-tuple-element.14.refs_2_, ...), custom_call_target="tpu_custom_call" | custom-call | tf_op jit(solution)/shard_map/emit/pallas_call | solution.py:678

commit v3 on v2

--- a/solution.py
+++ b/solution.py
@@ -19,7 +19,7 @@
 def kernel(
     nf, ns, image_ref, text_ref, weight_ref, up_ref, text_up_ref, qg_ref, kg_ref,
     image_out, text_out, weight_out, gain_out,
-    tokens, weights, ups, triple, grads, qn_s, kn_s, knt_s, dq_s, dk_s, dv_s,
+    tokens, weights, ups, triple, grads, qn_s, kn_s, knt_s, dk_s, dv_s, e_s, dp_s, p_s, ds_s,
     sib_send, sib_recv, mine, line_send, line_recv, w_send, w_recv, gain_all, gain_rows,
     text_share, text_sib_send, text_sib_recv, text_send, text_recv, tokens_t,
     x_send, x_recv, u_send, u_recv, wg_send, wg_recv, sb_send, sb_recv,
@@ -192,27 +192,43 @@
             w_wait(q, 0)
             w_wait(q, 1)
 
-    u_count = []
-
-    def u_launch(to_z, to_core, h, where=None):
+    def u_launch(to_z, to_core, h, slot, where=None):
         column = (to_z * 2 + to_core) * own_width + h * head
         copy = remote(
             up_ref.at[:, pl.ds(pl.multiple_of(column, head), head)],
             ups.at[pl.ds(place(to_z, z, core), rows), pl.ds(h * head, head)],
-            u_send.at[len(u_count)],
+            u_send.at[h, slot],
             u_recv.at[h, rank(to_z, z) * 2 + core],
             (f, to_z * 2 + to_core),
         )
-        u_count.append(0)
         launch(copy, where)
 
-    def send_upstream():
+    def send_upstream(late):
         for h in range(heads):
-            u_launch(z, other, h)
+            if not late:
+                u_launch(z, other, h, 0)
             for d in range(1, nz):
-                for which in (core, other):
-                    u_launch(z + d, which, h, where=z + d < nz)
-                    u_launch(z - d, which, h, where=z - d >= 0)
+                for to_z, exists, side in ((z + d, z + d < nz, 0), (z - d, z - d >= 0, 2)):
+                    if d > 1:
+                        outer = (to_z == 0) | (to_z == nz - 1)
+                        exists = exists & (outer if late else ~outer)
+                    elif late:
+                        continue
+                    for flip, which in enumerate((core, other)):
+                        u_launch(to_z, which, h, 4 * d - 3 + side + flip, where=exists)
+
+    factor = 1.0 / math.sqrt(head)
+    query_gain = qg_ref[...]
+    key_gain = kg_ref[...]
+    block = e_s.shape[1]
+    per_block = block // rows
+    text_pieces = text_rows // rows
+
+    def columns(c, h):
+        return pl.ds(c * own_width + h * head, head)
+
+    def inverse_of(values):
+        return lax.rsqrt(jnp.mean(values * values, axis=-1, keepdims=True) + EPSILON)
 
     def transpose(start, count):
         at = pl.ds(start, count)
@@ -223,6 +239,17 @@
         triple[at, :] = jnp.dot(
             tokens[at, :], weights[...], preferred_element_type=F32
         ).astype(BF16)
+        for h in range(heads):
+            for r in range(start, start + count, rows):
+                at = pl.ds(r, rows)
+                qf = triple[at, columns(0, h)].astype(F32)
+                qn_s[h, at, :] = (qf * inverse_of(qf) * query_gain).astype(BF16)
+                kf = triple[at, columns(1, h)].astype(F32)
+                kn = kf * inverse_of(kf) * key_gain
+                kn_s[h, at, :] = kn.astype(BF16)
+                knt_s[h, :, at] = kn.T.astype(BF16)
+                dk_s[h, at, :] = jnp.zeros((rows, head), F32)
+                dv_s[h, at, :] = jnp.zeros((rows, head), F32)
 
     pair = 2 * rows
     first = text_rows + pair
@@ -257,23 +284,11 @@
             for source, exists, onward, onward_ok in sides:
                 pl.when(exists)(functools.partial(x_wait, source, other, ch))
         if d == max(1, nz - 2):
-            send_upstream()
+            send_upstream(False)
+    send_upstream(True)
     last = first + (nz - 2) * pair
     transpose(last, pair)
     project(last, pair)
-
-    factor = 1.0 / math.sqrt(head)
-    query_gain = qg_ref[...]
-    key_gain = kg_ref[...]
-    block = max(b for b in range(128, 385, 128) if length % b == 0)
-    per_block = block // rows
-    text_pieces = text_rows // rows
-
-    def columns(c, h):
-        return pl.ds(c * own_width + h * head, head)
-
-    def inverse_of(values):
-        return lax.rsqrt(jnp.mean(values * values, axis=-1, keepdims=True) + EPSILON)
 
     def rms_backward(values, gain, incoming):
         inverse = inverse_of(values)
@@ -287,52 +302,63 @@
         remote(
             up_ref.at[:, pl.ds(0, head)],
             ups.at[at, pl.ds(h * head, head)],
-            u_send.at[0], u_recv.at[h, j], (f, s),
+            u_send.at[0, 0], u_recv.at[h, j], (f, s),
         ).wait_recv()
+
+    scale = factor * math.log2(math.e)
+    step = 128
+
+    def folded(values):
+        return jnp.sum(values.reshape(-1, 8, values.shape[1]), axis=0)
 
     gain_q = jnp.zeros((1, head), F32)
     gain_k = jnp.zeros((1, head), F32)
     for h in range(heads):
-        qf = triple[:, columns(0, h)].astype(F32)
-        qn_s[...] = (qf * inverse_of(qf) * query_gain).astype(BF16)
-        kf = triple[:, columns(1, h)].astype(F32)
-        kn = (kf * inverse_of(kf) * key_gain).astype(BF16)
-        kn_s[...] = kn
-        knt_s[...] = kn.astype(F32).T.astype(BF16)
-        dk_s[...] = jnp.zeros_like(dk_s)
-        dv_s[...] = jnp.zeros_like(dv_s)
-
         def visit(i, carry, h=h):
             for jj in range(per_block):
                 j = i * per_block + jj - text_pieces
                 pl.when((j >= 0) & (j != core))(functools.partial(u_wait, h, j))
             at = pl.ds(pl.multiple_of(i * block, block), block)
-            queries = qn_s[at, :]
+            queries = qn_s[h, at, :]
             upstream = ups[at, pl.ds(h * head, head)]
-            scores = lax.dot_general(kn_s[...], queries, NT, preferred_element_type=F32)
-            p = jnp.exp(scores * factor)
-            p = p * (1.0 / jnp.sum(p, axis=0, keepdims=True))
-            dp = lax.dot_general(
-                triple[:, columns(2, h)], upstream, NT, preferred_element_type=F32
+            total = jnp.zeros((8, block), F32)
+            dots = jnp.zeros((8, block), F32)
+            for r in range(0, length, length):
+                keys = pl.ds(r, length)
+                scores = lax.dot_general(kn_s[h, keys, :], queries, NT, preferred_element_type=F32)
+                e = jnp.exp2(scores * scale)
+                e_s[keys, :] = e
+                dp = lax.dot_general(
+                    triple[keys, columns(2, h)], upstream, NT, preferred_element_type=F32
+                )
+                dp_s[keys, :] = dp
+                total += folded(e)
+                dots += folded(e * dp)
+            inverse = 1.0 / jnp.sum(total, axis=0, keepdims=True)
+            dot = jnp.sum(dots, axis=0, keepdims=True) * inverse
+            for r in range(0, length, step):
+                keys = pl.ds(r, step)
+                p = e_s[keys, :] * inverse
+                p_s[keys, :] = p.astype(BF16)
+                ds_s[keys, :] = (p * (dp_s[keys, :] - dot)).astype(BF16)
+            dv_s[h] += jnp.dot(p_s[...], upstream, preferred_element_type=F32)
+            dk_s[h] += jnp.dot(ds_s[...], queries, preferred_element_type=F32)
+            dqn = jnp.dot(knt_s[h], ds_s[...], preferred_element_type=F32).T * factor
+            dq, part = rms_backward(triple[at, columns(0, h)].astype(F32), query_gain, dqn)
+            grads[at, columns(0, h)] = dq.astype(BF16)
+            return carry + part
+
+        gain_q = lax.fori_loop(0, length // block, visit, gain_q)
+        for r in range(0, length, step):
+            at = pl.ds(r, step)
+            dk, part = rms_backward(
+                triple[at, columns(1, h)].astype(F32), key_gain, dk_s[h, at, :] * factor
             )
-            dot = jnp.sum(p * dp, axis=0, keepdims=True)
-            ds = (p * (dp - dot)).astype(BF16)
-            dv_s[...] += jnp.dot(p.astype(BF16), upstream, preferred_element_type=F32)
-            dk_s[...] += jnp.dot(ds, queries, preferred_element_type=F32)
-            dq_s[at, :] = jnp.dot(knt_s[...], ds, preferred_element_type=F32).T * factor
-            return carry
-
-        lax.fori_loop(0, length // block, visit, 0)
-        dq, part = rms_backward(triple[:, columns(0, h)].astype(F32), query_gain, dq_s[...])
-        gain_q += part
-        grads[:, columns(0, h)] = dq.astype(BF16)
-        dk, part = rms_backward(
-            triple[:, columns(1, h)].astype(F32), key_gain, dk_s[...] * factor
-        )
-        gain_k += part
-        grads[:, columns(1, h)] = dk.astype(BF16)
-        grads[:, columns(2, h)] = dv_s[...].astype(BF16)
-
+            gain_k += part
+            grads[at, columns(1, h)] = dk.astype(BF16)
+            grads[at, columns(2, h)] = dv_s[h, at, :].astype(BF16)
+
+    early = len(pending)
     gain_all[s, 0:1, :] = gain_q
     gain_all[s, 1:2, :] = gain_k
     for k in range(1, ns):
@@ -545,6 +571,14 @@
             t_wait(index)
             t_copy(index, z, other, nz + o).start()
 
+    def drain(items):
+        for where, copy in items:
+            if where is None:
+                copy.wait_send()
+            else:
+                pl.when(where)(copy.wait_send)
+
+    drain(pending[:early])
     finish(0)
     for q in targets:
         remote(
@@ -567,11 +601,7 @@
     for o in range(2):
         t_wait(o * 2 + other)
 
-    for where, copy in pending:
-        if where is None:
-            copy.wait_send()
-        else:
-            pl.when(where)(copy.wait_send)
+    drain(pending[early:])
     for ch in range(CHUNKS):
         for k in range(nz - 1):
             pl.when(ends)(line_copy(ordered(k), ch, jnp.where(z == 0, 1, nz - 2)).wait_send)
@@ -615,6 +645,7 @@
     nz = ns // 2
     width3 = three * own_width
     piece = text_rows // 4
+    block = max(b for b in range(128, 385, 128) if length % b == 0)
     vmem = pl.BlockSpec(memory_space=pltpu.VMEM)
     hbm = pl.BlockSpec(memory_space=pl.ANY)
     dma = pltpu.SemaphoreType.DMA
@@ -634,12 +665,15 @@
             pltpu.VMEM((length, own_width), BF16),
             pltpu.VMEM((length, width3), BF16),
             pltpu.VMEM((length, width3), BF16),
-            pltpu.VMEM((length, head), BF16),
-            pltpu.VMEM((length, head), BF16),
-            pltpu.VMEM((head, length), BF16),
-            pltpu.VMEM((length, head), F32),
-            pltpu.VMEM((length, head), F32),
-            pltpu.VMEM((length, head), F32),
+            pltpu.VMEM((heads, length, head), BF16),
+            pltpu.VMEM((heads, length, head), BF16),
+            pltpu.VMEM((heads, head, length), BF16),
+            pltpu.VMEM((heads, length, head), F32),
+            pltpu.VMEM((heads, length, head), F32),
+            pltpu.VMEM((length, block), F32),
+            pltpu.VMEM((length, block), F32),
+            pltpu.VMEM((length, block), BF16),
+            pltpu.VMEM((length, block), BF16),
             pltpu.VMEM((nz, rows, depth), BF16),
             pltpu.VMEM((nz, rows, depth), BF16),
             pltpu.VMEM((nz, rows, depth), F32),
@@ -656,7 +690,7 @@
             pltpu.VMEM((2, 2, piece, depth), BF16),
             pltpu.VMEM((depth, length), BF16),
             dma((3 * CHUNKS + 4 * (nz - 1) * CHUNKS,)), dma((ns, CHUNKS)),
-            dma((heads * (1 + 4 * (nz - 1)),)), dma((heads, ns)),
+            dma((heads, 1 + 4 * (nz - 1))), dma((heads, ns)),
             dma((2 + 4 * (nf // 2 - 1),)), dma((nf, 2)),
             dma((nz,)), dma((nz,)),
             dma((nz, CHUNKS)), dma((nz + 1, CHUNKS)),

time: 90.9 us -> 87.3 us (0.960); the launches traced: 89.4 us -> 86.8 us
  Pallas kernels: 88.6 us -> 86 us
    pallas_call x1, Pallas kernels: 87.3 us -> 84.7 us  [local(): pl.pallas_call(functools.partial(kernel, nf, ns), out_shape=(pltpu.VMEM((...]
where the time goes in v3:
time: 87.3 us; the launch traced here: 86.8 us
  Pallas kernels  86 us (99%)
    pallas_call x1, Pallas kernels, local(): pl.pallas_call(functools.partial(kernel, nf, ns), out_shape=(pltpu.VMEM((...  84.7 us

profile of v3, /device:TPU:1, one launch (start us, length us, event | category | flops | bytes accessed | tf_op | source)
XLA Modules:
  0.0 86.8 jit_solution(11171568649705641590)
XLA Ops:
  0.6 84.7 %joint_backward.1 = (bf16[128,1536]{1,0:T(8,128)(2,1)S(1)}, bf16[128,1536]{1,0:T(8,128)(2,1)S(1)}, f32[3,384,256]{2,1,0:T(8,128)S(1)}, f32[2,128]{1,0:T(2,128)S(1)}) custom-call(bf16[128,1536]{1,0:T(8,128)(2,1)} %bitcast.13, bf16[128,1536]{1,0:T(8,128)(2,1)} %bitcast.14, bf16[3,384,2048]{2,1,0:T(8,128)(2,1)} %bitcast.10, bf16[128,2048]{1,0:T(8,128)(2,1)} %bitcast.11, ...), custom_call_target="tpu_custom_call" | custom-call | tf_op jit(solution)/shard_map/joint_backward/pallas_call | solution.py:652
  85.4 1.3 %emit.1 = (bf16[128,1536]{1,0:T(8,128)(2,1)}, bf16[128,1536]{1,0:T(8,128)(2,1)}, f32[3,384,256]{2,1,0:T(8,128)}, f32[2,128]{1,0:T(2,128)}) custom-call(bf16[128,1536]{1,0:T(8,128)(2,1)S(1)} %get-tuple-element.12.refs_0_, bf16[128,1536]{1,0:T(8,128)(2,1)S(1)} %get-tuple-element.13.refs_1_, f32[3,384,256]{2,1,0:T(8,128)S(1)} %get-tuple-element.14.refs_2_, ...), custom_call_target="tpu_custom_call" | custom-call | tf_op jit(solution)/shard_map/emit/pallas_call | solution.py:712
